TPU v7x, 32 devices: a whole 2x2x4 slice. The times are simulated.
32 devices in a mesh: space: 16 (over z, y, core), lat: 2 (over x).
Axes of the slice: x: 2, y: 2, z: 4, core: 2. Of those that a mesh axis runs over, the one named last changes fastest.
Arguments:
- fields: bfloat16 [4, 64, 3, 65536], P(None, None, None, ('space', 'lat')), may hold values from -6 to 6
- cell_latent: int32 [65536], P(('space', 'lat')), may hold values from 0 to 1023, as said below
- enc_weight: float32 [3, 65536], P(None, ('space', 'lat')), may hold values from -0.4375 to 0.4375
- dec_weight: float32 [3, 65536], P(None, ('space', 'lat')), may hold values from -5 to 5
- trans_weight: bfloat16 [1024, 64, 5120], P(('space', 'lat')), may hold values from -0.15625 to 0.15625
- graph_logits: float32 [1024, 5120], P(('space', 'lat')), may hold values from -6 to 6
- hidden_bias: float32 [1024, 64], P(('space', 'lat')), may hold values from -3 to 3
- out_weight: float32 [1024, 64], P(('space', 'lat')), may hold values from -0.75 to 0.75
- noise_var: float32 [1024], P(('space', 'lat')), may hold values from 0.005 to 0.05
Outputs:
- grad_enc: float32 [3, 65536], P(None, ('space', 'lat'))
- grad_dec: float32 [3, 65536], P(None, ('space', 'lat'))
- grad_trans: bfloat16 [1024, 64, 5120], P(('space', 'lat'))
- grad_graph: float32 [1024, 5120], P(('space', 'lat'))
Inputs may be any that keep to these rules, and one draw needn't show every extreme that they name: `cell_latent`: cells d * 2048 to (d + 1) * 2048 - 1 are assigned latents from (d - 1) * 32 to (d + 2) * 32 - 1; for every d other than the first, the first of these cells has a latent below d * 32, and for every d other than the last, the last has one at (d + 1) * 32 or above.
All inputs are finite; a program needn't handle non-finite values.
Results may differ from a plain program's by a relative error of at most 0.0023.
The roundings to bfloat16 on the way count: a program that leaves them out, or rounds other values in their place, can miss the bound.
Values may be sent and summed in bfloat16 or wider, within the bound.
No kernel may reach another device: no remote copies, remote signals or barrier semaphores. Data moves between devices by JAX's collectives and lax.ppermute only.
A program may use at most 192 MiB of HBM per device.

v0:
```python
import jax
import jax.numpy as jnp
from jax import lax
from jax.sharding import PartitionSpec as P

LAGS = 5
sparsity_weight = 0.01


def shifted(block, axis, distance):
    devices = range(lax.axis_size(axis))
    route = [(i - distance, i) for i in devices if i - distance in devices]
    return lax.ppermute(block, axis, route)


def extended(block, sides, width):
    for axis, dim in sides:
        count = lax.axis_size(axis)
        forward = [(i, i + 1) for i in range(count - 1)]
        backward = [(target, source) for source, target in forward]
        low = lax.ppermute(
            lax.slice_in_dim(block, block.shape[dim] - width, None, axis=dim), axis, forward
        )
        high = lax.ppermute(lax.slice_in_dim(block, 0, width, axis=dim), axis, backward)
        block = jnp.concatenate([low, block, high], axis=dim)
    return block


def body(
    fields,
    cell_latent,
    enc_weight,
    dec_weight,
    trans_weight,
    graph_logits,
    hidden_bias,
    out_weight,
    noise_var,
):
    batch_size, step_count, var_count, cell_count = fields.shape
    lat_dev, hidden, lag_width = trans_weight.shape
    latent_count = lag_width // LAGS
    highest = lax.Precision.HIGHEST
    device = lax.axis_index(("space", "lat"))
    norm_factor = 1.0 / (batch_size * step_count)
    rows = batch_size * (step_count - LAGS)
    local_index = cell_latent - (device - 1) * lat_dev
    one_hot = (local_index[:, None] == jnp.arange(3 * lat_dev, dtype=jnp.int32)[None, :]).astype(
        jnp.float32
    )
    projected = jnp.sum(fields.astype(jnp.float32) * enc_weight[None, None], axis=2)
    enc_part = jnp.einsum("btc,cj->btj", projected, one_hot, precision=highest)
    spread_table = jnp.zeros((batch_size, step_count, latent_count + 2 * lat_dev), jnp.float32)
    spread_table = lax.dynamic_update_slice_in_dim(spread_table, enc_part, device * lat_dev, 2)
    latent_full = lax.psum(spread_table[:, :, lat_dev : latent_count + lat_dev], ("space", "lat"))
    own_latent = lax.dynamic_slice_in_dim(latent_full, device * lat_dev, lat_dev, 2)
    latent_bf = latent_full.astype(jnp.bfloat16)
    padded_latent = jnp.pad(latent_bf, ((0, 0), (0, 0), (lat_dev, lat_dev)))
    window = lax.dynamic_slice_in_dim(padded_latent, device * lat_dev, 3 * lat_dev, 2)
    cell_values = jnp.einsum("btj,cj->btc", window.astype(jnp.float32), one_hot, precision=highest)
    resid = dec_weight[None, None] * cell_values[:, :, None, :] - fields.astype(jnp.float32)
    grad_dec = norm_factor * jnp.einsum("btvc,btc->vc", resid, cell_values, precision=highest)
    cell_grad = norm_factor * jnp.sum(resid * dec_weight[None, None], axis=2)
    window_grad = jnp.einsum("btc,cj->btj", cell_grad, one_hot, precision=highest)
    lagged = jnp.stack(
        [latent_bf[:, LAGS - lag : step_count - lag, :] for lag in range(1, LAGS + 1)], axis=2
    )
    lagged = lagged.reshape(rows, lag_width)
    edge_prob = jax.nn.sigmoid(graph_logits)
    eff_weight = (trans_weight.astype(jnp.float32) * edge_prob[:, None, :]).astype(jnp.bfloat16)
    pre_act = (
        jnp.einsum("ri,kmi->rkm", lagged, eff_weight, preferred_element_type=jnp.float32)
        + hidden_bias[None]
    )
    gate_sig = jax.nn.sigmoid(pre_act)
    predicted = jnp.sum(pre_act * gate_sig * out_weight[None], axis=2)
    target = own_latent[:, LAGS:, :].reshape(rows, lat_dev)
    direct = norm_factor * (target - predicted) / noise_var[None]
    hidden_grad = (
        (-direct)[:, :, None] * out_weight[None] * gate_sig * (1.0 + pre_act * (1.0 - gate_sig))
    )
    hidden_bf = hidden_grad.astype(jnp.bfloat16)
    weight_grad = jnp.einsum("rkm,ri->kmi", hidden_bf, lagged, preferred_element_type=jnp.float32)
    grad_trans = (weight_grad * edge_prob[:, None, :]).astype(jnp.bfloat16)
    flip = edge_prob * (1.0 - edge_prob)
    grad_graph = (
        jnp.sum(weight_grad * trans_weight.astype(jnp.float32), axis=1) * flip
        + sparsity_weight * flip
    )
    input_grad = jnp.einsum(
        "rkm,kmi->ri", hidden_bf, eff_weight, preferred_element_type=jnp.float32
    )
    input_grad = input_grad.reshape(batch_size, step_count - LAGS, LAGS, latent_count)
    owned_terms = lax.psum_scatter(input_grad, ("space", "lat"), scatter_dimension=3, tiled=True)
    lag_grad = jnp.zeros((batch_size, step_count, lat_dev), jnp.float32)
    for lag in range(1, LAGS + 1):
        lag_grad = lag_grad + jnp.pad(
            owned_terms[:, :, lag - 1, :], ((0, 0), (LAGS - lag, lag), (0, 0))
        )
    grad_above = shifted(window_grad[:, :, :lat_dev], ("space", "lat"), -1)
    grad_below = shifted(window_grad[:, :, 2 * lat_dev :], ("space", "lat"), 1)
    direct_steps = jnp.pad(
        direct.reshape(batch_size, step_count - LAGS, lat_dev), ((0, 0), (LAGS, 0), (0, 0))
    )
    own_grad = (
        window_grad[:, :, lat_dev : 2 * lat_dev] + grad_above + grad_below + lag_grad + direct_steps
    )
    halo_grad = extended(own_grad, ((("space", "lat"), 2),), lat_dev)
    cell_total = jnp.einsum("btj,cj->btc", halo_grad, one_hot, precision=highest)
    grad_enc = jnp.einsum("btvc,btc->vc", fields.astype(jnp.float32), cell_total, precision=highest)
    return (grad_enc, grad_dec, grad_trans, grad_graph)


def solution(mesh):
    return jax.shard_map(
        body,
        mesh=mesh,
        in_specs=(
            P(None, None, None, ("space", "lat")),
            P(("space", "lat")),
            P(None, ("space", "lat")),
            P(None, ("space", "lat")),
            P(("space", "lat"), None, None),
            P(("space", "lat"), None),
            P(("space", "lat"), None),
            P(("space", "lat"), None),
            P(("space", "lat")),
        ),
        out_specs=(
            P(None, ("space", "lat")),
            P(None, ("space", "lat")),
            P(("space", "lat"), None, None),
            P(("space", "lat"), None),
        ),
        check_vma=False,
    )
```

profile of v0, /device:TPU:1, one launch (start us, length us, event | category | flops | bytes accessed | tf_op | source)
XLA Modules:
  0.0 460.4 jit_solution(15953483216375521314)
XLA Ops:
  7.2 0.7 broadcast_subtract_fusion
  7.9 2.8 fusion.9
  10.7 1.2 fusion.18
  11.9 0.1 broadcast_in_dim.2
  12.0 1.1 dynamic_update_slice.3
  13.1 1.3 slice.60
  14.5 0.2 add_divide_fusion.1
  14.7 131.0 %all-reduce.11.cloned.1.call-done = f32[4,64,1024]{2,1,0:T(8,128)} async-done(((f32[4,64,1024]{2,1,0:T(8,128)}), f32[4,64,1024]{2,1,0:T(8,128)}) %all-reduce.11.cloned.1.call-update) | async-done | bytes 1048592 | tf_op jit(solution)/shard_map/psum | solution.py:55
  145.7 1.4 convert_element_type.38
  147.2 0.5 fusion.16
  147.7 0.1 fusion.25
  147.8 0.1 copy-done
  147.9 1.1 multiply_reduce_fusion.2
  149.1 1.2 fusion.10
  150.3 0.8 fusion.43
  151.0 3.1 collective-permute-start.1
  154.1 3.3 collective-permute-start
  157.5 0.1 fusion.24
  157.6 0.1 fusion.23
  157.7 0.1 fusion.22
  157.9 3.4 copy.19
  161.3 6.8 %reshape.55 = bf16[236,5120,1]{1,0,2:T(8,128)(2,1)} reshape(bf16[4,59,5,1024]{3,2,1,0:T(8,128)(2,1)} %copy.19) | data formatting | bytes 4833280 | tf_op jit(solution)/shard_map/reshape | solution.py:68
  168.1 12.6 %multiply_reduce_fusion.3 = (f32[236,32]{0,1:T(8,128)}, f32[236,32,64]{0,2,1:T(8,128)}) fusion(f32[32,64]{1,0:T(8,128)} %param.16, f32[32,64]{1,0:T(8,128)} %param.15, bf16[236,5120,1]{1,0,2:T(8,128)(2,1)} %reshape.55, bf16[32,64,5120]{2,1,0:T(8,128)(2,1)} %param.13, f32[32,5120]{1,0:T(8,128)S(1)} %add_divide_fusion.1), kind=kOutput, calls=%fused_computation.16 | convolution fusion | flops 4984111616 | bytes 26023424 | tf_op jit(solution)/shard_map/ri,kmi->rkm/dot_general | solution.py:72
  180.7 1.5 reduce_sum.41
  182.1 1.6 copy.26
  183.8 1.8 multiply_divide_fusion
  185.5 1.6 copy.18
  187.2 1.5 reshape.51
  188.7 1.5 divide_negate_fusion
  190.2 16.1 %fusion.6 = f32[236,5120]{1,0:T(8,128)} fusion(bf16[32,64,5120]{2,1,0:T(8,128)(2,1)} %param.13, f32[32,5120]{1,0:T(8,128)S(1)} %add_divide_fusion.1, f32[236,32,64]{0,2,1:T(8,128)} %get-tuple-element.18, f32[236,32]{0,1:T(8,128)} %divide_negate_fusion, f32[32,64]{1,0:T(8,128)} %param.16, f32[32,64]{1,0:T(8,128)} %param.15), kind=kOutput, calls=%fused_computation.9 | convolution fusion | flops 4986052608 | bytes 28440064 | tf_op jit(solution)/shard_map/rkm,kmi->ri/dot_general | solution.py:90
  206.3 7.5 %reshape.53 = f32[4,59,5,1024]{3,2,1,0:T(8,128)} reshape(f32[236,5120]{1,0:T(8,128)} %fusion.6) | data formatting | bytes 9666560 | tf_op jit(solution)/shard_map/reshape | solution.py:93
  213.8 10.4 %copy.20 = f32[4,59,5,1024]{1,0,2,3:T(4,128)} copy(f32[4,59,5,1024]{3,2,1,0:T(8,128)} %reshape.53) | data formatting | bytes 9666560 | tf_op jit(solution)/shard_map/reshape | solution.py:93
  224.2 23.0 %fusion.1 = (f32[32,5120]{1,0:T(8,128)}, bf16[32,64,5120]{2,1,0:T(8,128)(2,1)}) fusion(bf16[32,64,5120]{2,1,0:T(8,128)(2,1)} %param.13, f32[32,5120]{1,0:T(8,128)S(1)} %add_divide_fusion.1, bf16[236,5120,1]{1,0,2:T(8,128)(2,1)} %reshape.55, f32[236,32,64]{0,2,1:T(8,128)} %get-tuple-element.18, f32[236,32]{0,1:T(8,128)} %divide_negate_fusion, ...), kind=kOutput, calls=%fused_computation.3 | convolution fusion | flops 5006860288 | bytes 47650304 | tf_op jit(solution)/shard_map/rkm,ri->kmi/dot_general | solution.py:83
  247.2 179.6 %all-reduce.13.cloned.1.call-done = f32[4,59,5,1024]{1,0,2,3:T(4,128)} async-done(((f32[4,59,5,1024]{1,0,2,3:T(4,128)}), f32[4,59,5,1024]{1,0,2,3:T(4,128)}) %all-reduce.13.cloned.1.call-update) | async-done | bytes 4833296
  426.8 1.7 constant_dynamic-slice_fusion.3
  428.6 1.6 copy.45
  430.1 1.6 copy.44
  431.8 1.6 copy.43
  433.4 1.6 copy.42
  435.0 1.6 copy.41
  436.6 1.4 fusion.32
  438.0 4.0 collective-permute-start.3
  442.0 1.9 collective-permute-start.2
  444.0 1.0 fusion.20
  445.0 4.7 %collective-permute-done.2 = f32[4,64,32]{2,1,0:T(8,128)S(1)} collective-permute-done((f32[4,64,32]{2,1,0:T(8,128)S(1)}, f32[4,64,32]{2,1,0:T(8,128)S(1)}, u32[]{:S(2)}, u32[]{:S(2)}) %collective-permute-start.2) | collective-permute-done | bytes 32800 | tf_op jit(solution)/shard_map/ppermute | solution.py:21
  449.7 1.0 convolution_bitcast_fusion
  450.7 2.2 multiply_reduce_fusion
  452.9 0.6 multiply_bitcast_fusion
  (21 shorter events, 0.2 us)
Async XLA Ops:
  7.2 138.6 %all-reduce.11.cloned.1.call-start = ((), (), s32[]{:S(2)}) async-start(), calls=%async_computation | async-start | bytes 2097152 | tf_op jit(solution)/shard_map/psum | solution.py:55
  11.9 2.6 copy-start.2
  14.5 412.4 %all-reduce.13.cloned.1.call-start = ((), (), s32[]{:S(2)}) async-start(), calls=%async_computation.1 | async-start | bytes 20971520
  14.7 133.1 %copy-start.4 = (f32[3,2048]{1,0:T(4,128)S(1)}, f32[3,2048]{1,0:T(4,128)}, u32[]{:S(2)}) copy-start(f32[3,2048]{1,0:T(4,128)} %param.12) | copy-start | bytes 73732
  145.7 2.2 copy-start
  151.0 285.5 %collective-permute-start.1 = (f32[4,64,32]{2,1,0:T(8,128)}, f32[4,64,32]{2,1,0:T(8,128)}, u32[]{:S(2)}, u32[]{:S(2)}) collective-permute-start(f32[4,64,32]{2,1,0:T(8,128)} %get-tuple-element.16), channel_id=1, source_target_pairs={{0,1},{1,2},{2,3},{3,4},{4,5},{5,6},{6,7},{7,8},{8,9},{9,10},{10,1... | collective-permute-start | bytes 98312 | tf_op jit(solution)/shard_map/ppermute | solution.py:13
  154.1 282.5 %collective-permute-start = (f32[4,64,32]{2,1,0:T(8,128)}, f32[4,64,32]{2,1,0:T(8,128)}, u32[]{:S(2)}, u32[]{:S(2)}) collective-permute-start(f32[4,64,32]{2,1,0:T(8,128)} %get-tuple-element.15), channel_id=1, source_target_pairs={{1,0},{2,1},{3,2},{4,3},{5,4},{6,5},{7,6},{8,7},{9,8},{10,9},{11,1... | collective-permute-start | bytes 98312 | tf_op jit(solution)/shard_map/ppermute | solution.py:13
  168.1 15.7 %copy-start.6 = (f32[32]{0:T(128)S(1)}, f32[32]{0:T(128)}, u32[]{:S(2)}) copy-start(f32[32]{0:T(128)} %param.17) | copy-start | bytes 388
  247.2 196.8 %copy-start.3 = (f32[32,5120]{1,0:T(8,128)S(1)}, f32[32,5120]{1,0:T(8,128)}, u32[]{:S(2)}) copy-start(f32[32,5120]{1,0:T(8,128)} %get-tuple-element.8) | copy-start | bytes 1966084
  438.0 12.7 %copy-start.1 = (bf16[4,64,3,2048]{3,1,2,0:T(8,128)(2,1)S(1)}, bf16[4,64,3,2048]{3,1,2,0:T(8,128)(2,1)}, u32[]{:S(2)}) copy-start(bf16[4,64,3,2048]{3,1,2,0:T(8,128)(2,1)} %param.9) | copy-start | bytes 9437188
  438.0 12.7 %copy-start.5 = (f32[3,2048]{1,0:T(4,128)S(1)}, f32[3,2048]{1,0:T(4,128)}, u32[]{:S(2)}) copy-start(f32[3,2048]{1,0:T(4,128)} %param.12) | copy-start | bytes 73732
  438.0 7.0 %collective-permute-start.3 = (f32[4,64,32]{2,1,0:T(8,128)S(1)}, f32[4,64,32]{2,1,0:T(8,128)S(1)}, u32[]{:S(2)}, u32[]{:S(2)}) collective-permute-start(f32[4,64,32]{2,1,0:T(8,128)S(1)} %fusion.32), channel_id=1, source_target_pairs={{1,0},{2,1},{3,2},{4,3},{5,4},{6,5},{7,6},{8,7},{9,8},{10,9},{11,1... | collective-permute-start | bytes 98312 | tf_op jit(solution)/shard_map/ppermute | solution.py:24
  442.0 7.6 %collective-permute-start.2 = (f32[4,64,32]{2,1,0:T(8,128)S(1)}, f32[4,64,32]{2,1,0:T(8,128)S(1)}, u32[]{:S(2)}, u32[]{:S(2)}) collective-permute-start(f32[4,64,32]{2,1,0:T(8,128)S(1)} %fusion.32), channel_id=1, source_target_pairs={{0,1},{1,2},{2,3},{3,4},{4,5},{5,6},{6,7},{7,8},{8,9},{9,10},{10,1... | collective-permute-start | bytes 98312 | tf_op jit(solution)/shard_map/ppermute | solution.py:21
Sparse Core Ops, SparseCore 0:
  14.6 131.1 all-reduce.10
  224.4 202.4 all-reduce.12
where the time goes:
time: 462 us; the launch traced here: 460 us
  waiting for transfers between devices  315 us (68%)
  matrix products  55.6 us (12%)
  local copies, waits for them, and re-layouts  48 us (10%)
  other arithmetic  14.7 us (3%)
  between operations  14.3 us (3%)
  starting transfers between devices  12.4 us (3%)
    unnamed x3, waiting for transfers between devices  180 us
    psum x1, waiting for transfers between devices, body(): lax.psum(spread_table[:, :, lat_dev:latent_count + lat_dev], ('space', 'l...  131 us
    dot_general x1, matrix products, body(): jnp.einsum('rkm,ri->kmi', hidden_bf, lagged, preferred_element_type=jnp.f...  23 us
    reshape x2, local copies, waits for them, and re-layouts, body(): input_grad.reshape(batch_size, step_count - LAGS, LAGS, latent_count)  17.9 us
    dot_general x1, matrix products, body(): jnp.einsum('rkm,kmi->ri', hidden_bf, eff_weight, preferred_element_type=j...  16.1 us
    dot_general x1, matrix products, body(): jnp.einsum('ri,kmi->rkm', lagged, eff_weight, preferred_element_type=jnp....  12.6 us
  transfers between devices with their start and end apart: 6, of which 3 were waited for; matrix products, arithmetic and copies ran while one was open for 22% of the time, Pallas kernels for 0%

commit v1 on v0

--- a/solution.py
+++ b/solution.py
@@ -52,7 +52,10 @@
     enc_part = jnp.einsum("btc,cj->btj", projected, one_hot, precision=highest)
     spread_table = jnp.zeros((batch_size, step_count, latent_count + 2 * lat_dev), jnp.float32)
     spread_table = lax.dynamic_update_slice_in_dim(spread_table, enc_part, device * lat_dev, 2)
-    latent_full = lax.psum(spread_table[:, :, lat_dev : latent_count + lat_dev], ("space", "lat"))
+    latent_full = jnp.sum(
+        lax.all_gather(spread_table[:, :, lat_dev : latent_count + lat_dev], ("space", "lat")),
+        axis=0,
+    )
     own_latent = lax.dynamic_slice_in_dim(latent_full, device * lat_dev, lat_dev, 2)
     latent_bf = latent_full.astype(jnp.bfloat16)
     padded_latent = jnp.pad(latent_bf, ((0, 0), (0, 0), (lat_dev, lat_dev)))

time: 462 us -> 525 us (1.14)
  waiting for transfers between devices: 315 us -> 377 us
  other arithmetic: 14.7 us -> 25.3 us
  local copies, waits for them, and re-layouts: 48 us -> 40.4 us
    all_gather x0 -> x1, waiting for transfers between devices: none -> 196 us  [body(): lax.all_gather(spread_table[:, :, lat_dev:latent_count + lat_dev], ('spac...]
    psum x1 -> x0, waiting for transfers between devices: 131 us -> none  [body(): lax.psum(spread_table[:, :, lat_dev:latent_count + lat_dev], ('space', 'l...]
    reduce_sum x0 -> x1, other arithmetic: none -> 11.9 us  [body(): jnp.sum(lax.all_gather(spread_table[:, :, lat_dev:latent_count + lat_dev]...]
  transfers between devices with their start and end apart: 6 -> 6, of which waited for: 3 -> 3; matrix products, arithmetic and copies ran while one was open for 22% -> 17% of each run, Pallas kernels for 0% -> 0%
where the time goes in v1:
time: 525 us; the launch traced here: 524 us
  waiting for transfers between devices  377 us (72%)
  matrix products  55.4 us (11%)
  local copies, waits for them, and re-layouts  40.4 us (8%)
  other arithmetic  25.3 us (5%)
  between operations  14.3 us (3%)
  starting transfers between devices  11.6 us (2%)
    all_gather x1, waiting for transfers between devices, body(): lax.all_gather(spread_table[:, :, lat_dev:latent_count + lat_dev], ('spac...  196 us
    unnamed x3, waiting for transfers between devices  177 us
    dot_general x1, matrix products, body(): jnp.einsum('rkm,ri->kmi', hidden_bf, lagged, preferred_element_type=jnp.f...  23.3 us
    reshape x2, local copies, waits for them, and re-layouts, body(): input_grad.reshape(batch_size, step_count - LAGS, LAGS, latent_count)  17.9 us
    dot_general x1, matrix products, body(): jnp.einsum('rkm,kmi->ri', hidden_bf, eff_weight, preferred_element_type=j...  16.2 us
    dot_general x1, matrix products, body(): jnp.einsum('ri,kmi->rkm', lagged, eff_weight, preferred_element_type=jnp....  12 us
    reduce_sum x1, other arithmetic, body(): jnp.sum(lax.all_gather(spread_table[:, :, lat_dev:latent_count + lat_dev]...  11.9 us
  transfers between devices with their start and end apart: 6, of which 3 were waited for; matrix products, arithmetic and copies ran while one was open for 17% of the time, Pallas kernels for 0%

profile of v1, /device:TPU:1, one launch (start us, length us, event | category | flops | bytes accessed | tf_op | source)
XLA Modules:
  0.0 524.0 jit_solution(13015529915717454145)
XLA Ops:
  7.2 0.7 broadcast_subtract_fusion
  7.9 2.8 fusion.9
  10.7 1.2 fusion.18
  12.0 1.1 dynamic_update_slice.3
  13.1 1.3 slice.60
  14.5 1.0 add_divide_fusion.1
  15.5 196.4 %all-gather.3.cloned.1.call-done = f32[128,64,1024]{2,1,0:T(8,128)} async-done(((f32[4,64,1024]{2,1,0:T(8,128)}), f32[128,64,1024]{2,1,0:T(8,128)}) %all-gather.3.cloned.1.call-update) | async-done | bytes 33554448 | tf_op jit(solution)/shard_map/all_gather | solution.py:56
  211.9 11.9 %reduce_sum.48 = f32[4,64,1024]{2,1,0:T(8,128)S(1)} reduce(f32[32,4,64,1024]{3,2,1,0:T(8,128)} %bitcast.51, f32[]{:T(128)} %constant.13.clone.1), dimensions={0}, to_apply=%region_1.0 | reduce | flops 8126464 | bytes 34603012 | tf_op jit(solution)/shard_map/reduce_sum | solution.py:55
  223.9 0.5 fusion.16
  224.4 0.1 fusion.25
  224.5 1.1 copy-done
  225.7 1.1 multiply_reduce_fusion.2
  226.8 1.2 fusion.10
  228.0 0.8 fusion.43
  228.8 3.0 collective-permute-start.1
  231.8 2.5 collective-permute-start
  234.4 0.1 fusion.24
  234.5 0.1 fusion.23
  234.6 0.1 fusion.22
  234.8 3.4 copy.19
  238.2 6.7 %reshape.56 = bf16[236,5120,1]{1,0,2:T(8,128)(2,1)} reshape(bf16[4,59,5,1024]{3,2,1,0:T(8,128)(2,1)} %copy.19) | data formatting | bytes 4833280 | tf_op jit(solution)/shard_map/reshape | solution.py:71
  245.0 12.0 %multiply_reduce_fusion.3 = (f32[236,32]{0,1:T(8,128)S(1)}, f32[236,32,64]{0,2,1:T(8,128)}) fusion(f32[32,64]{1,0:T(8,128)S(1)} %copy-done.9, f32[32,64]{1,0:T(8,128)S(1)} %copy-done.11, bf16[236,5120,1]{1,0,2:T(8,128)(2,1)} %reshape.56, bf16[32,64,5120]{2,1,0:T(8,128)(2,1)} %param.13, f32[32,5120]{1,0:T(8,128)} %add_divide_fusion.1), kind=kOutput, calls=%fused_computation.16 | convolution fusion | flops 4984111616 | bytes 26023424 | tf_op jit(solution)/shard_map/ri,kmi->rkm/dot_general | solution.py:75
  257.0 0.1 reduce_sum.51
  257.1 0.5 copy-done.7
  257.6 0.1 copy.26
  257.8 0.8 multiply_divide_fusion
  258.5 1.0 copy.18
  259.6 0.8 divide_negate_fusion
  260.5 16.2 %fusion.6 = f32[236,5120]{1,0:T(8,128)} fusion(bf16[32,64,5120]{2,1,0:T(8,128)(2,1)} %param.13, f32[32,5120]{1,0:T(8,128)} %add_divide_fusion.1, f32[236,32,64]{0,2,1:T(8,128)} %get-tuple-element.18, f32[236,32]{0,1:T(8,128)S(1)} %divide_negate_fusion, f32[32,64]{1,0:T(8,128)} %param.16, f32[32,64]{1,0:T(8,128)} %param.15), kind=kOutput, calls=%fused_computation.9 | convolution fusion | flops 4986052608 | bytes 28440064 | tf_op jit(solution)/shard_map/rkm,kmi->ri/dot_general | solution.py:93
  276.6 7.5 %reshape.53 = f32[4,59,5,1024]{3,2,1,0:T(8,128)} reshape(f32[236,5120]{1,0:T(8,128)} %fusion.6) | data formatting | bytes 9666560 | tf_op jit(solution)/shard_map/reshape | solution.py:96
  284.2 10.4 %copy.20 = f32[4,59,5,1024]{1,0,2,3:T(4,128)} copy(f32[4,59,5,1024]{3,2,1,0:T(8,128)} %reshape.53) | data formatting | bytes 9666560 | tf_op jit(solution)/shard_map/reshape | solution.py:96
  294.6 1.1 copy-done.4
  295.6 23.3 %fusion.1 = (f32[32,5120]{1,0:T(8,128)}, bf16[32,64,5120]{2,1,0:T(8,128)(2,1)}) fusion(bf16[32,64,5120]{2,1,0:T(8,128)(2,1)} %param.13, f32[32,5120]{1,0:T(8,128)S(1)} %copy-done.4, bf16[236,5120,1]{1,0,2:T(8,128)(2,1)} %reshape.56, f32[236,32,64]{0,2,1:T(8,128)} %get-tuple-element.18, f32[236,32]{0,1:T(8,128)S(1)} %divide_negate_fusion, ...), kind=kOutput, calls=%fused_computation.3 | convolution fusion | flops 5006860288 | bytes 47650304 | tf_op jit(solution)/shard_map/rkm,ri->kmi/dot_general | solution.py:86
  319.0 177.0 %all-reduce.10.cloned.1.call-done = f32[4,59,5,1024]{1,0,2,3:T(4,128)} async-done(((f32[4,59,5,1024]{1,0,2,3:T(4,128)}), f32[4,59,5,1024]{1,0,2,3:T(4,128)}) %all-reduce.10.cloned.1.call-update) | async-done | bytes 4833296
  496.0 1.6 constant_dynamic-slice_fusion.3
  497.6 0.1 copy.45
  497.7 0.1 copy.44
  497.9 1.0 copy.43
  498.8 0.8 copy.42
  499.6 0.8 copy.41
  500.4 1.2 fusion.32
  501.6 4.0 collective-permute-start.3
  505.7 1.9 collective-permute-start.2
  507.6 2.1 fusion.20
  509.7 3.6 collective-permute-done.2
  513.3 1.0 convolution_bitcast_fusion
  514.4 2.2 multiply_reduce_fusion
  516.6 0.6 multiply_bitcast_fusion
  (34 shorter events, 0.4 us)
Async XLA Ops:
  7.2 204.8 %all-gather.3.cloned.1.call-start = ((), (), s32[]{:S(2)}) async-start(), calls=%async_computation | async-start | bytes 34603008 | tf_op jit(solution)/shard_map/all_gather | solution.py:56
  11.9 2.6 copy-start.2
  14.5 481.6 %all-reduce.10.cloned.1.call-start = ((), (), s32[]{:S(2)}) async-start(), calls=%async_computation.1 | async-start | bytes 20971520
  223.8 1.9 copy-start
  223.8 1.9 copy-start.5
  228.8 271.6 %collective-permute-start.1 = (f32[4,64,32]{2,1,0:T(8,128)}, f32[4,64,32]{2,1,0:T(8,128)}, u32[]{:S(2)}, u32[]{:S(2)}) collective-permute-start(f32[4,64,32]{2,1,0:T(8,128)} %get-tuple-element.16), channel_id=1, source_target_pairs={{0,1},{1,2},{2,3},{3,4},{4,5},{5,6},{6,7},{7,8},{8,9},{9,10},{10,1... | collective-permute-start | bytes 98312 | tf_op jit(solution)/shard_map/ppermute | solution.py:13
  231.8 268.6 %collective-permute-start = (f32[4,64,32]{2,1,0:T(8,128)}, f32[4,64,32]{2,1,0:T(8,128)}, u32[]{:S(2)}, u32[]{:S(2)}) collective-permute-start(f32[4,64,32]{2,1,0:T(8,128)} %get-tuple-element.15), channel_id=1, source_target_pairs={{1,0},{2,1},{3,2},{4,3},{5,4},{6,5},{7,6},{8,7},{9,8},{10,9},{11,1... | collective-permute-start | bytes 98312 | tf_op jit(solution)/shard_map/ppermute | solution.py:13
  238.2 6.8 %copy-start.9 = (f32[32,64]{1,0:T(8,128)S(1)}, f32[32,64]{1,0:T(8,128)}, u32[]{:S(2)}) copy-start(f32[32,64]{1,0:T(8,128)} %param.16) | copy-start | bytes 24580
  238.2 6.8 %copy-start.11 = (f32[32,64]{1,0:T(8,128)S(1)}, f32[32,64]{1,0:T(8,128)}, u32[]{:S(2)}) copy-start(f32[32,64]{1,0:T(8,128)} %param.15) | copy-start | bytes 24580
  245.0 12.8 %copy-start.8 = (f32[32]{0:T(128)S(1)}, f32[32]{0:T(128)}, u32[]{:S(2)}) copy-start(f32[32]{0:T(128)} %param.17) | copy-start | bytes 388
  257.0 0.6 copy-start.7
  294.6 1.1 copy-start.4
  294.6 1.1 copy-start.10
  294.6 1.1 copy-start.12
  319.0 188.6 %copy-start.3 = (f32[32,5120]{1,0:T(8,128)S(1)}, f32[32,5120]{1,0:T(8,128)}, u32[]{:S(2)}) copy-start(f32[32,5120]{1,0:T(8,128)} %param.14) | copy-start | bytes 1966084
  501.6 12.7 %copy-start.1 = (bf16[4,64,3,2048]{3,1,2,0:T(8,128)(2,1)S(1)}, bf16[4,64,3,2048]{3,1,2,0:T(8,128)(2,1)}, u32[]{:S(2)}) copy-start(bf16[4,64,3,2048]{3,1,2,0:T(8,128)(2,1)} %param.9) | copy-start | bytes 9437188
  501.6 12.7 %copy-start.6 = (f32[3,2048]{1,0:T(4,128)S(1)}, f32[3,2048]{1,0:T(4,128)}, u32[]{:S(2)}) copy-start(f32[3,2048]{1,0:T(4,128)} %param.12) | copy-start | bytes 73732
  501.6 8.1 %collective-permute-start.3 = (f32[4,64,32]{2,1,0:T(8,128)S(1)}, f32[4,64,32]{2,1,0:T(8,128)S(1)}, u32[]{:S(2)}, u32[]{:S(2)}) collective-permute-start(f32[4,64,32]{2,1,0:T(8,128)S(1)} %fusion.32), channel_id=1, source_target_pairs={{1,0},{2,1},{3,2},{4,3},{5,4},{6,5},{7,6},{8,7},{9,8},{10,9},{11,1... | collective-permute-start | bytes 98312 | tf_op jit(solution)/shard_map/ppermute | solution.py:24
  505.7 7.6 %collective-permute-start.2 = (f32[4,64,32]{2,1,0:T(8,128)S(1)}, f32[4,64,32]{2,1,0:T(8,128)S(1)}, u32[]{:S(2)}, u32[]{:S(2)}) collective-permute-start(f32[4,64,32]{2,1,0:T(8,128)S(1)} %fusion.32), channel_id=1, source_target_pairs={{0,1},{1,2},{2,3},{3,4},{4,5},{5,6},{6,7},{7,8},{8,9},{9,10},{10,1... | collective-permute-start | bytes 98312 | tf_op jit(solution)/shard_map/ppermute | solution.py:21
Sparse Core Ops, SparseCore 0:
  14.6 197.2 all-gather.2
  294.7 201.2 all-reduce.9
